TPU v7x, 32 devices: a whole 2x2x4 slice. The times are simulated.
32 devices in a mesh: local: 4 (over y, x), dp: 8 (over z, core).
Axes of the slice: x: 2, y: 2, z: 4, core: 2. Of those that a mesh axis runs over, the one named last changes fastest.
Arguments:
- gradient: bfloat16 [32, 72, 7168], P(('local', 'dp')), may hold values from -1.1953125 to 1.1953125
- feedback: bfloat16 [32, 72, 7168], P(('local', 'dp')), may hold values from -0.59765625 to 0.59765625
- basis_in: float32 [7168, 32], replicated, may hold values from -6 to 6
Outputs:
- new_feedback: bfloat16 [32, 72, 7168], P(('local', 'dp'))
- new_basis: float32 [7168, 32], replicated
All inputs are finite; a program needn't handle non-finite values.
Results may differ from a plain program's by a relative error of at most 0.001.
Values sent between devices are 32-bit elements; how exact they have to be, the bound alone decides.
No kernel may reach another device: no remote copies, remote signals or barrier semaphores. Data moves between devices by JAX's collectives and lax.ppermute only.
A program may use at most 64 MiB of HBM per device.

v0:
```python
import jax
import jax.numpy as jnp
from jax import lax
from jax.sharding import PartitionSpec as P

epsilon = 1e-06


def orthonormal(matrix):
    highest = lax.Precision.HIGHEST
    count = matrix.shape[1]
    positions = jnp.arange(count, dtype=jnp.int32)

    def sweep(index, working):
        vector = lax.dynamic_slice_in_dim(working, index, 1, 1)[:, 0]
        vector = vector * lax.rsqrt(jnp.sum(vector * vector) + epsilon)
        projections = jnp.dot(vector, working, precision=highest)
        projections = jnp.where(positions > index, projections, jnp.zeros_like(projections))
        working = working - vector[:, None] * projections[None, :]
        return lax.dynamic_update_slice_in_dim(working, vector[:, None], index, 1)

    return lax.fori_loop(0, count, sweep, matrix)


def body(gradient, feedback, basis_in):
    highest = lax.Precision.HIGHEST
    merged = gradient[0].astype(jnp.float32) + feedback[0].astype(jnp.float32)
    workers = lax.axis_size("local") * lax.axis_size("dp")
    left_term = jnp.dot(merged, basis_in, precision=highest)
    left_sum = lax.psum(left_term, ("local", "dp"))
    left_basis = orthonormal(left_sum)
    right_term = jnp.dot(merged.T, left_basis, precision=highest)
    share_rows = lax.psum_scatter(right_term, "local", scatter_dimension=0, tiled=True)
    share_rows = lax.psum(share_rows, "dp")
    new_basis = lax.all_gather(share_rows, "local", axis=0, tiled=True)
    approx = jnp.dot(left_basis, new_basis.T, precision=highest) / workers
    new_feedback = (merged - approx).astype(jnp.bfloat16)
    return (new_feedback[None], new_basis)


def solution(mesh):
    return jax.shard_map(
        body,
        mesh=mesh,
        in_specs=(P(("local", "dp"), None, None), P(("local", "dp"), None, None), P()),
        out_specs=(P(("local", "dp"), None, None), P()),
        check_vma=False,
    )
```

profile of v0, /device:TPU:0, one launch (start us, length us, event | category | flops | bytes accessed | tf_op | source)
XLA Modules:
  0.0 214.8 jit_solution(16565798836019193358)
XLA Ops:
  7.2 1.1 copy-done
  8.3 3.4 %fusion.8 = f32[72,32]{0,1:T(8,128)S(1)} fusion(f32[7168,32]{0,1:T(8,128)S(1)} %copy-done, bf16[1,72,7168]{2,1,0:T(8,128)(2,1)} %param.6, bf16[1,72,7168]{2,1,0:T(8,128)(2,1)} %param.5), kind=kOutput, calls=%fused_computation.13 | convolution fusion | flops 199729152 | bytes 2991104 | tf_op jit(solution)/shard_map/dot_general | solution.py:29
  11.7 42.1 %psum.14 = f32[72,32]{0,1:T(8,128)S(1)} all-reduce(f32[72,32]{0,1:T(8,128)S(1)} %fusion.8), channel_id=1, replica_groups=mesh['local'=4,'dp'=8] {'local','dp'}, use_global_device_ids=true, to_apply=%region_0.0 | all-reduce | flops 2304 | bytes 18432 | tf_op jit(solution)/shard_map/psum | solution.py:30
  53.8 50.7 %while.14 = (s32[]{:T(128)}, f32[72,32]{0,1:T(8,128)S(1)}, s32[]{:T(128)}, f32[]{:T(128)}, s32[]{:T(128)}) while((s32[]{:T(128)}, f32[72,32]{0,1:T(8,128)S(1)}, s32[]{:T(128)}, f32[]{:T(128)}, s32[]{:T(128)}) %tuple.35), condition=%wide.region_3.4_spmd.clone, body=%wide.region_1.3_spmd.clone.sunk | while | flops 32610 | bytes 30609 | solution.py:22
  55.4 0.6 multiply_reduce_fusion.2
  57.0 0.6 multiply_reduce_fusion.2
  58.6 0.6 multiply_reduce_fusion.2
  60.1 0.6 multiply_reduce_fusion.2
  61.7 0.6 multiply_reduce_fusion.2
  63.3 0.6 multiply_reduce_fusion.2
  64.9 0.6 multiply_reduce_fusion.2
  66.5 0.6 multiply_reduce_fusion.2
  68.1 0.6 multiply_reduce_fusion.2
  69.6 0.6 multiply_reduce_fusion.2
  71.2 0.6 multiply_reduce_fusion.2
  72.8 0.6 multiply_reduce_fusion.2
  74.4 0.6 multiply_reduce_fusion.2
  77.6 0.6 multiply_reduce_fusion.2
  79.2 0.6 multiply_reduce_fusion.2
  82.3 0.6 multiply_reduce_fusion.2
  85.5 0.6 multiply_reduce_fusion.2
  88.7 0.6 multiply_reduce_fusion.2
  91.8 0.6 multiply_reduce_fusion.2
  93.4 0.6 multiply_reduce_fusion.2
  95.0 0.6 multiply_reduce_fusion.2
  102.9 0.6 multiply_reduce_fusion.2
  104.5 2.4 %fusion.6 = f32[7168,32]{0,1:T(8,128)} fusion(f32[72,32]{0,1:T(8,128)S(1)} %get-tuple-element.66, bf16[1,72,7168]{2,1,0:T(8,128)(2,1)S(1)} %copy-done.1, bf16[1,72,7168]{2,1,0:T(8,128)(2,1)S(1)} %copy-done.2), kind=kOutput, calls=%fused_computation.11 | convolution fusion | flops 199729152 | bytes 2991104 | tf_op jit(solution)/shard_map/dot_general | solution.py:32
  107.0 27.0 %reduce-scatter.2.cloned.1.call-done = f32[1792,32]{0,1:T(8,128)} async-done(((f32[7168,32]{0,1:T(8,128)}), f32[1792,32]{0,1:T(8,128)}) %reduce-scatter.2.cloned.1.call-update) | async-done | bytes 229392 | tf_op jit(solution)/shard_map/reduce_scatter | solution.py:33
  134.1 55.3 %all-reduce.2.cloned.1.call-done = f32[1792,32]{0,1:T(8,128)} async-done(((f32[1792,32]{0,1:T(8,128)}), f32[1792,32]{0,1:T(8,128)}) %all-reduce.2.cloned.1.call-update) | async-done | bytes 229392 | tf_op jit(solution)/shard_map/psum | solution.py:34
  189.4 14.7 %all_gather.3 = f32[7168,32]{0,1:T(8,128)S(1)} all-gather(f32[1792,32]{0,1:T(8,128)} %all-reduce.2.cloned.1.call-done), channel_id=1, replica_groups=mesh['local'=4,'dp'=8] {'local'}, dimensions={0}, use_global_device_ids=true | all-gather | bytes 1146880 | tf_op jit(solution)/shard_map/all_gather | solution.py:35
  204.1 2.9 %fusion.5 = bf16[1,72,7168]{2,1,0:T(8,128)(2,1)} fusion(f32[72,32]{0,1:T(8,128)S(1)} %get-tuple-element.66, f32[7168,32]{0,1:T(8,128)S(1)} %all_gather.3, bf16[1,72,7168]{2,1,0:T(8,128)(2,1)S(1)} %copy-done.1, bf16[1,72,7168]{2,1,0:T(8,128)(2,1)S(1)} %copy-done.2), kind=kOutput, calls=%fused_computation.10 | convolution fusion | flops 201277440 | bytes 4023296 | tf_op jit(solution)/shard_map/dot_general | solution.py:36
  207.0 0.9 copy.14
  (179 shorter events, 14.7 us)
Async XLA Ops:
  7.2 1.2 copy-start
  7.2 97.3 %copy-start.2 = (bf16[1,72,7168]{2,1,0:T(8,128)(2,1)S(1)}, bf16[1,72,7168]{2,1,0:T(8,128)(2,1)}, u32[]{:S(2)}) copy-start(bf16[1,72,7168]{2,1,0:T(8,128)(2,1)} %param.5) | copy-start | bytes 3096580
  7.2 97.3 %copy-start.1 = (bf16[1,72,7168]{2,1,0:T(8,128)(2,1)S(1)}, bf16[1,72,7168]{2,1,0:T(8,128)(2,1)}, u32[]{:S(2)}) copy-start(bf16[1,72,7168]{2,1,0:T(8,128)(2,1)} %param.6) | copy-start | bytes 3096580
  7.2 126.8 %reduce-scatter.2.cloned.1.call-start = ((), (), s32[]{:S(2)}) async-start(), calls=%async_computation.1 | async-start | bytes 1146880 | tf_op jit(solution)/shard_map/reduce_scatter | solution.py:33
  107.0 82.4 %all-reduce.2.cloned.1.call-start = ((), (), s32[]{:S(2)}) async-start(), calls=%async_computation.2 | async-start | bytes 458752 | tf_op jit(solution)/shard_map/psum | solution.py:34
Sparse Core Ops, SparseCore 0:
  107.1 26.8 reduce-scatter.1
  136.4 52.9 all-reduce.1
where the time goes:
time: 215 us
  waiting for transfers between devices  82.3 us (38%)
  blocking collectives  56.8 us (26%)
  other arithmetic  22.9 us (11%)
  loops' own time  22.8 us (11%)
  between operations  14.1 us (7%)
  matrix products  12.9 us (6%)
  local copies, waits for them, and re-layouts  2.95 us (1%)
    psum x1, waiting for transfers between devices, body(): share_rows = lax.psum(share_rows, 'dp')  55.3 us
    psum x1, blocking collectives, body(): left_sum = lax.psum(left_term, ('local', 'dp'))  42.1 us
    reduce_scatter x1, waiting for transfers between devices, body(): lax.psum_scatter(right_term, 'local', scatter_dimension=0, tiled=True)  27 us
    another operation x1, loops' own time, orthonormal(): return lax.fori_loop(0, count, sweep, matrix)  22.8 us
    reduce_sum x32, other arithmetic, sweep(): vector = vector * lax.rsqrt(jnp.sum(vector * vector) + epsilon)  19.4 us
    all_gather x1, blocking collectives, body(): new_basis = lax.all_gather(share_rows, 'local', axis=0, tiled=True)  14.7 us
  transfers between devices with their start and end apart: 2, of which 2 were waited for; matrix products, arithmetic and copies ran while one was open for 0% of the time, Pallas kernels for 0%

commit v1 on v0

--- a/solution.py
+++ b/solution.py
@@ -4,6 +4,17 @@
 from jax.sharding import PartitionSpec as P
 
 epsilon = 1e-06
+
+
+def pass_along(array, name, d):
+    size = lax.axis_size(name)
+    right = [(i, (i + 1) % size) for i in range(size)]
+    terms = [array]
+    for stride in range(1, size):
+        terms = [lax.ppermute(terms[0], name, right), *terms]
+    result = jnp.concatenate(terms, axis=d)
+    shift = (lax.axis_index(name) + 1) * terms[-1].shape[d]
+    return jnp.roll(result, shift, axis=d)
 
 
 def orthonormal(matrix):
@@ -32,7 +43,7 @@
     right_term = jnp.dot(merged.T, left_basis, precision=highest)
     share_rows = lax.psum_scatter(right_term, "local", scatter_dimension=0, tiled=True)
     share_rows = lax.psum(share_rows, "dp")
-    new_basis = lax.all_gather(share_rows, "local", axis=0, tiled=True)
+    new_basis = pass_along(share_rows, "local", 0)
     approx = jnp.dot(left_basis, new_basis.T, precision=highest) / workers
     new_feedback = (merged - approx).astype(jnp.bfloat16)
     return (new_feedback[None], new_basis)

time: 215 us -> 230 us (1.070)
  waiting for transfers between devices: 82.3 us -> 105 us
  blocking collectives: 56.8 us -> 42.1 us
  local copies, waits for them, and re-layouts: 2.95 us -> 7.18 us
    ppermute x0 -> x3, waiting for transfers between devices: none -> 22.8 us  [pass_along(): terms = [lax.ppermute(terms[0], name, right), *terms]]
    all_gather x1 -> x0, blocking collectives: 14.7 us -> none  [body(): new_basis = lax.all_gather(share_rows, 'local', axis=0, tiled=True)]
    unnamed x7 -> x17, local copies, waits for them, and re-layouts: 2.04 us -> 5.94 us
  transfers between devices with their start and end apart: 2 -> 5, of which waited for: 2 -> 5; matrix products, arithmetic and copies ran while one was open for 0% -> 0% of each run, Pallas kernels for 0% -> 0%
where the time goes in v1:
time: 230 us; the launch traced here: 229 us
  waiting for transfers between devices  105 us (46%)
  blocking collectives  42.1 us (18%)
  other arithmetic  22.9 us (10%)
  loops' own time  22.8 us (10%)
  between operations  14.1 us (6%)
  matrix products  12.9 us (6%)
  local copies, waits for them, and re-layouts  7.18 us (3%)
    psum x1, waiting for transfers between devices, body(): share_rows = lax.psum(share_rows, 'dp')  55.3 us
    psum x1, blocking collectives, body(): left_sum = lax.psum(left_term, ('local', 'dp'))  42.1 us
    reduce_scatter x1, waiting for transfers between devices, body(): lax.psum_scatter(right_term, 'local', scatter_dimension=0, tiled=True)  27 us
    another operation x1, loops' own time, orthonormal(): return lax.fori_loop(0, count, sweep, matrix)  22.8 us
    ppermute x3, waiting for transfers between devices, pass_along(): terms = [lax.ppermute(terms[0], name, right), *terms]  22.8 us
    reduce_sum x32, other arithmetic, sweep(): vector = vector * lax.rsqrt(jnp.sum(vector * vector) + epsilon)  19.4 us
    unnamed x17, local copies, waits for them, and re-layouts  5.94 us
  transfers between devices with their start and end apart: 5, of which 5 were waited for; matrix products, arithmetic and copies ran while one was open for 0% of the time, Pallas kernels for 0%

profile of v1, /device:TPU:0, one launch (start us, length us, event | category | flops | bytes accessed | tf_op | source)
XLA Modules:
  0.0 229.2 jit_solution(12756359186477263850)
XLA Ops:
  7.2 1.1 copy-done
  8.3 3.4 %fusion.8 = f32[72,32]{0,1:T(8,128)S(1)} fusion(f32[7168,32]{0,1:T(8,128)S(1)} %copy-done, bf16[1,72,7168]{2,1,0:T(8,128)(2,1)} %param.6, bf16[1,72,7168]{2,1,0:T(8,128)(2,1)} %param.5), kind=kOutput, calls=%fused_computation.13 | convolution fusion | flops 199729152 | bytes 2991104 | tf_op jit(solution)/shard_map/dot_general | solution.py:40
  11.7 42.1 %psum.14 = f32[72,32]{0,1:T(8,128)S(1)} all-reduce(f32[72,32]{0,1:T(8,128)S(1)} %fusion.8), channel_id=1, replica_groups=mesh['local'=4,'dp'=8] {'local','dp'}, use_global_device_ids=true, to_apply=%region_0.0 | all-reduce | flops 2304 | bytes 18432 | tf_op jit(solution)/shard_map/psum | solution.py:41
  53.8 50.7 %while.14 = (s32[]{:T(128)}, f32[72,32]{0,1:T(8,128)S(1)}, s32[]{:T(128)}, f32[]{:T(128)}, s32[]{:T(128)}) while((s32[]{:T(128)}, f32[72,32]{0,1:T(8,128)S(1)}, s32[]{:T(128)}, f32[]{:T(128)}, s32[]{:T(128)}) %tuple.35), condition=%wide.region_3.4_spmd.clone, body=%wide.region_1.3_spmd.clone.sunk | while | flops 32610 | bytes 30609 | solution.py:33
  55.4 0.6 multiply_reduce_fusion.2
  57.0 0.6 multiply_reduce_fusion.2
  60.1 0.6 multiply_reduce_fusion.2
  63.3 0.6 multiply_reduce_fusion.2
  66.5 0.6 multiply_reduce_fusion.2
  68.1 0.6 multiply_reduce_fusion.2
  74.4 0.6 multiply_reduce_fusion.2
  76.0 0.6 multiply_reduce_fusion.2
  77.6 0.6 multiply_reduce_fusion.2
  85.5 0.6 multiply_reduce_fusion.2
  88.7 0.6 multiply_reduce_fusion.2
  91.8 0.6 multiply_reduce_fusion.2
  99.8 0.6 multiply_reduce_fusion.2
  101.3 0.6 multiply_reduce_fusion.2
  102.9 0.6 multiply_reduce_fusion.2
  104.5 2.4 %fusion.6 = f32[7168,32]{0,1:T(8,128)} fusion(f32[72,32]{0,1:T(8,128)S(1)} %get-tuple-element.66, bf16[1,72,7168]{2,1,0:T(8,128)(2,1)S(1)} %copy-done.1, bf16[1,72,7168]{2,1,0:T(8,128)(2,1)S(1)} %copy-done.2), kind=kOutput, calls=%fused_computation.11 | convolution fusion | flops 199729152 | bytes 2991104 | tf_op jit(solution)/shard_map/dot_general | solution.py:43
  107.0 27.0 %reduce-scatter.2.cloned.1.call-done = f32[1792,32]{0,1:T(8,128)} async-done(((f32[7168,32]{0,1:T(8,128)}), f32[1792,32]{0,1:T(8,128)}) %reduce-scatter.2.cloned.1.call-update) | async-done | bytes 229392 | tf_op jit(solution)/shard_map/reduce_scatter | solution.py:44
  134.1 55.3 %all-reduce.2.cloned.1.call-done = f32[1792,32]{0,1:T(8,128)} async-done(((f32[1792,32]{0,1:T(8,128)}), f32[1792,32]{0,1:T(8,128)}) %all-reduce.2.cloned.1.call-update) | async-done | bytes 229392 | tf_op jit(solution)/shard_map/psum | solution.py:45
  189.4 1.5 collective-permute-start
  190.9 7.7 %collective-permute-done = f32[1792,32]{0,1:T(8,128)S(1)} collective-permute-done((f32[1792,32]{0,1:T(8,128)}, f32[1792,32]{0,1:T(8,128)S(1)}, u32[]{:S(2)}, u32[]{:S(2)}) %collective-permute-start) | collective-permute-done | bytes 229408 | tf_op jit(solution)/shard_map/ppermute | solution.py:14
  199.1 7.6 %collective-permute-done.1 = f32[1792,32]{0,1:T(8,128)} collective-permute-done((f32[1792,32]{0,1:T(8,128)S(1)}, f32[1792,32]{0,1:T(8,128)}, u32[]{:S(2)}, u32[]{:S(2)}) %collective-permute-start.1) | collective-permute-done | bytes 229408 | tf_op jit(solution)/shard_map/ppermute | solution.py:14
  206.7 7.5 %collective-permute-done.2 = f32[1792,32]{0,1:T(8,128)} collective-permute-done((f32[1792,32]{0,1:T(8,128)}, f32[1792,32]{0,1:T(8,128)}, u32[]{:S(2)}, u32[]{:S(2)}) %collective-permute-start.2) | collective-permute-done | bytes 229408 | tf_op jit(solution)/shard_map/ppermute | solution.py:14
  214.2 1.0 constant_dynamic-update-slice_fusion.7
  215.2 1.0 constant_dynamic-update-slice_fusion.6
  216.1 1.0 constant_dynamic-update-slice_fusion.4
  217.1 1.0 constant_dynamic-update-slice_fusion.3
  218.1 1.0 constant_dynamic-update-slice_fusion.2
  219.4 3.0 %fusion.5 = bf16[1,72,7168]{2,1,0:T(8,128)(2,1)} fusion(f32[72,32]{0,1:T(8,128)S(1)} %get-tuple-element.66, f32[7168,32]{0,1:T(8,128)S(1)} %constant_dynamic-slice_fusion.1, bf16[1,72,7168]{2,1,0:T(8,128)(2,1)S(1)} %copy-done.1, bf16[1,72,7168]{2,1,0:T(8,128)(2,1)S(1)} %copy-done.2), kind=kOutput, calls=%fused_computation.10 | convolution fusion | flops 201277440 | bytes 4023296 | tf_op jit(solution)/shard_map/dot_general | solution.py:47
  (196 shorter events, 19.9 us)
Async XLA Ops:
  7.2 1.2 copy-start
  7.2 97.3 %copy-start.2 = (bf16[1,72,7168]{2,1,0:T(8,128)(2,1)S(1)}, bf16[1,72,7168]{2,1,0:T(8,128)(2,1)}, u32[]{:S(2)}) copy-start(bf16[1,72,7168]{2,1,0:T(8,128)(2,1)} %param.5) | copy-start | bytes 3096580
  7.2 97.3 %copy-start.1 = (bf16[1,72,7168]{2,1,0:T(8,128)(2,1)S(1)}, bf16[1,72,7168]{2,1,0:T(8,128)(2,1)}, u32[]{:S(2)}) copy-start(bf16[1,72,7168]{2,1,0:T(8,128)(2,1)} %param.6) | copy-start | bytes 3096580
  7.2 126.8 %reduce-scatter.2.cloned.1.call-start = ((), (), s32[]{:S(2)}) async-start(), calls=%async_computation.1 | async-start | bytes 1146880 | tf_op jit(solution)/shard_map/reduce_scatter | solution.py:44
  107.0 82.4 %all-reduce.2.cloned.1.call-start = ((), (), s32[]{:S(2)}) async-start(), calls=%async_computation.2 | async-start | bytes 458752 | tf_op jit(solution)/shard_map/psum | solution.py:45
  189.4 29.7 %copy-start.4 = (f32[1792,32]{0,1:T(8,128)S(1)}, f32[1792,32]{0,1:T(8,128)}, u32[]{:S(2)}) copy-start(f32[1792,32]{0,1:T(8,128)} %all-reduce.2.cloned.1.call-done) | copy-start | bytes 688132
  189.4 9.1 %collective-permute-start = (f32[1792,32]{0,1:T(8,128)}, f32[1792,32]{0,1:T(8,128)S(1)}, u32[]{:S(2)}, u32[]{:S(2)}) collective-permute-start(f32[1792,32]{0,1:T(8,128)} %all-reduce.2.cloned.1.call-done), channel_id=1, source_target_pairs={{0,8},{8,16},{16,24},{24,0},{1,9},{9,17},{17,25},{25,1},{2,10},{10... | collective-permute-start | bytes 688136 | tf_op jit(solution)/shard_map/ppermute | solution.py:14
  198.5 8.2 %collective-permute-start.1 = (f32[1792,32]{0,1:T(8,128)S(1)}, f32[1792,32]{0,1:T(8,128)}, u32[]{:S(2)}, u32[]{:S(2)}) collective-permute-start(f32[1792,32]{0,1:T(8,128)S(1)} %collective-permute-done), channel_id=1, source_target_pairs={{0,8},{8,16},{16,24},{24,0},{1,9},{9,17},{17,25},{25,1},{2,10},{10... | collective-permute-start | bytes 688136 | tf_op jit(solution)/shard_map/ppermute | solution.py:14
  206.7 7.5 %collective-permute-start.2 = (f32[1792,32]{0,1:T(8,128)}, f32[1792,32]{0,1:T(8,128)}, u32[]{:S(2)}, u32[]{:S(2)}) collective-permute-start(f32[1792,32]{0,1:T(8,128)} %collective-permute-done.1), channel_id=1, source_target_pairs={{0,8},{8,16},{16,24},{24,0},{1,9},{9,17},{17,25},{25,1},{2,10},{10... | collective-permute-start | bytes 688136 | tf_op jit(solution)/shard_map/ppermute | solution.py:14
  219.4 3.0 %copy-start.3 = (f32[7168,32]{0,1:T(8,128)}, f32[7168,32]{0,1:T(8,128)S(1)}, u32[]{:S(2)}) copy-start(f32[7168,32]{0,1:T(8,128)S(1)} %constant_dynamic-slice_fusion.1) | copy-start | bytes 2752516
Sparse Core Ops, SparseCore 0:
  107.1 26.8 reduce-scatter.1
  136.4 52.9 all-reduce.1

commit v2 on v0

--- a/solution.py
+++ b/solution.py
@@ -31,7 +31,8 @@
     left_basis = orthonormal(left_sum)
     right_term = jnp.dot(merged.T, left_basis, precision=highest)
     share_rows = lax.psum_scatter(right_term, "local", scatter_dimension=0, tiled=True)
-    share_rows = lax.psum(share_rows, "dp")
+    blocks = lax.all_gather(share_rows, "dp", axis=0, tiled=False)
+    share_rows = blocks.sum(axis=0)
     new_basis = lax.all_gather(share_rows, "local", axis=0, tiled=True)
     approx = jnp.dot(left_basis, new_basis.T, precision=highest) / workers
     new_feedback = (merged - approx).astype(jnp.bfloat16)

time: 215 us -> 190 us (0.88)
  waiting for transfers between devices: 82.3 us -> 55.6 us
    psum x1 -> x0, waiting for transfers between devices: 55.3 us -> none  [body(): share_rows = lax.psum(share_rows, 'dp')]
    all_gather x0 -> x1, waiting for transfers between devices: none -> 28.6 us  [body(): blocks = lax.all_gather(share_rows, 'dp', axis=0, tiled=False)]
where the time goes in v2:
time: 190 us
  waiting for transfers between devices  55.6 us (29%)
  blocking collectives  55.3 us (29%)
  loops' own time  23.3 us (12%)
  other arithmetic  23.2 us (12%)
  between operations  14.1 us (7%)
  matrix products  12.9 us (7%)
  local copies, waits for them, and re-layouts  5.07 us (3%)
    psum x1, blocking collectives, body(): left_sum = lax.psum(left_term, ('local', 'dp'))  42.1 us
    all_gather x1, waiting for transfers between devices, body(): blocks = lax.all_gather(share_rows, 'dp', axis=0, tiled=False)  28.6 us
    reduce_scatter x1, waiting for transfers between devices, body(): lax.psum_scatter(right_term, 'local', scatter_dimension=0, tiled=True)  27 us
    another operation x1, loops' own time, orthonormal(): return lax.fori_loop(0, count, sweep, matrix)  23.3 us
    reduce_sum x32, other arithmetic, sweep(): vector = vector * lax.rsqrt(jnp.sum(vector * vector) + epsilon)  19.4 us
    all_gather x1, blocking collectives, body(): new_basis = lax.all_gather(share_rows, 'local', axis=0, tiled=True)  13.2 us
    dot_general x32, matrix products, sweep(): projections = jnp.dot(vector, working, precision=highest)  4.11 us
    unnamed x8, local copies, waits for them, and re-layouts  4.1 us
  transfers between devices with their start and end apart: 2, of which 2 were waited for; matrix products, arithmetic and copies ran while one was open for 0% of the time, Pallas kernels for 0%

profile of v2, /device:TPU:0, one launch (start us, length us, event | category | flops | bytes accessed | tf_op | source)
XLA Modules:
  0.0 189.5 jit_solution(406086770879196655)
XLA Ops:
  7.2 1.1 copy-done
  8.3 3.4 %fusion.8 = f32[72,32]{0,1:T(8,128)S(1)} fusion(f32[7168,32]{0,1:T(8,128)S(1)} %copy-done, bf16[1,72,7168]{2,1,0:T(8,128)(2,1)} %param.6, bf16[1,72,7168]{2,1,0:T(8,128)(2,1)} %param.5), kind=kOutput, calls=%fused_computation.13 | convolution fusion | flops 199729152 | bytes 2991104 | tf_op jit(solution)/shard_map/dot_general | solution.py:29
  11.7 42.1 %psum.7 = f32[72,32]{0,1:T(8,128)S(1)} all-reduce(f32[72,32]{0,1:T(8,128)S(1)} %fusion.8), channel_id=1, replica_groups=mesh['local'=4,'dp'=8] {'local','dp'}, use_global_device_ids=true, to_apply=%region_0.0 | all-reduce | flops 2304 | bytes 18432 | tf_op jit(solution)/shard_map/psum | solution.py:30
  53.8 51.1 %while.14 = (s32[]{:T(128)}, f32[72,32]{0,1:T(8,128)S(1)}, s32[]{:T(128)}, f32[]{:T(128)}, s32[]{:T(128)}) while((s32[]{:T(128)}, f32[72,32]{0,1:T(8,128)S(1)}, s32[]{:T(128)}, f32[]{:T(128)}, s32[]{:T(128)}) %tuple.35), condition=%wide.region_3.4_spmd.clone, body=%wide.region_1.3_spmd.clone.sunk | while | flops 32610 | bytes 30617 | solution.py:22
  55.4 0.6 multiply_reduce_fusion.2
  57.0 0.6 multiply_reduce_fusion.2
  58.6 0.6 multiply_reduce_fusion.2
  60.2 0.6 multiply_reduce_fusion.2
  61.8 0.6 multiply_reduce_fusion.2
  63.4 0.6 multiply_reduce_fusion.2
  65.0 0.6 multiply_reduce_fusion.2
  66.6 0.6 multiply_reduce_fusion.2
  68.2 0.6 multiply_reduce_fusion.2
  69.8 0.6 multiply_reduce_fusion.2
  71.4 0.6 multiply_reduce_fusion.2
  73.0 0.6 multiply_reduce_fusion.2
  74.6 0.6 multiply_reduce_fusion.2
  76.2 0.6 multiply_reduce_fusion.2
  77.8 0.6 multiply_reduce_fusion.2
  81.0 0.6 multiply_reduce_fusion.2
  85.8 0.6 multiply_reduce_fusion.2
  88.9 0.6 multiply_reduce_fusion.2
  92.1 0.6 multiply_reduce_fusion.2
  96.9 0.6 multiply_reduce_fusion.2
  103.3 0.6 multiply_reduce_fusion.2
  104.9 2.4 %fusion.6 = f32[7168,32]{0,1:T(8,128)} fusion(f32[72,32]{0,1:T(8,128)S(1)} %get-tuple-element.66, bf16[1,72,7168]{2,1,0:T(8,128)(2,1)S(1)} %copy-done.1, bf16[1,72,7168]{2,1,0:T(8,128)(2,1)S(1)} %copy-done.2), kind=kOutput, calls=%fused_computation.11 | convolution fusion | flops 199729152 | bytes 2991104 | tf_op jit(solution)/shard_map/dot_general | solution.py:32
  107.4 27.0 %reduce-scatter.2.cloned.1.call-done = f32[1792,32]{0,1:T(8,128)} async-done(((f32[7168,32]{0,1:T(8,128)}), f32[1792,32]{0,1:T(8,128)}) %reduce-scatter.2.cloned.1.call-update) | async-done | bytes 229392 | tf_op jit(solution)/shard_map/reduce_scatter | solution.py:33
  134.5 28.6 %all-gather.3.cloned.1.call-done = f32[14336,32]{0,1:T(8,128)} async-done(((f32[1792,32]{0,1:T(8,128)}), f32[14336,32]{0,1:T(8,128)}) %all-gather.3.cloned.1.call-update) | async-done | bytes 1835024 | tf_op jit(solution)/shard_map/all_gather | solution.py:34
  163.1 2.1 %copy.5 = f32[4,8,8,1792]{3,2,1,0:T(8,128)S(1)} copy(f32[4,8,8,1792]{3,1,2,0:T(8,128)} %bitcast.33) | data formatting | bytes 3670016
  165.6 13.2 %all_gather.11 = f32[7168,32]{0,1:T(8,128)S(1)} all-gather(f32[1792,32]{0,1:T(8,128)S(1)} %bitcast_reduce_fusion), channel_id=1, replica_groups=mesh['local'=4,'dp'=8] {'local'}, dimensions={0}, use_global_device_ids=true | all-gather | bytes 1146880 | tf_op jit(solution)/shard_map/all_gather | solution.py:36
  178.8 2.9 %fusion.5 = bf16[1,72,7168]{2,1,0:T(8,128)(2,1)} fusion(f32[72,32]{0,1:T(8,128)S(1)} %get-tuple-element.66, f32[7168,32]{0,1:T(8,128)S(1)} %all_gather.11, bf16[1,72,7168]{2,1,0:T(8,128)(2,1)S(1)} %copy-done.1, bf16[1,72,7168]{2,1,0:T(8,128)(2,1)S(1)} %copy-done.2), kind=kOutput, calls=%fused_computation.10 | convolution fusion | flops 201277440 | bytes 4023296 | tf_op jit(solution)/shard_map/dot_general | solution.py:37
  181.7 0.9 copy.14
  (181 shorter events, 15.6 us)
Async XLA Ops:
  7.2 1.2 copy-start
  7.2 97.7 %copy-start.1 = (bf16[1,72,7168]{2,1,0:T(8,128)(2,1)S(1)}, bf16[1,72,7168]{2,1,0:T(8,128)(2,1)}, u32[]{:S(2)}) copy-start(bf16[1,72,7168]{2,1,0:T(8,128)(2,1)} %param.6) | copy-start | bytes 3096580
  7.2 97.7 %copy-start.2 = (bf16[1,72,7168]{2,1,0:T(8,128)(2,1)S(1)}, bf16[1,72,7168]{2,1,0:T(8,128)(2,1)}, u32[]{:S(2)}) copy-start(bf16[1,72,7168]{2,1,0:T(8,128)(2,1)} %param.5) | copy-start | bytes 3096580
  7.2 127.3 %reduce-scatter.2.cloned.1.call-start = ((), (), s32[]{:S(2)}) async-start(), calls=%async_computation.1 | async-start | bytes 1146880 | tf_op jit(solution)/shard_map/reduce_scatter | solution.py:33
  107.4 55.7 %all-gather.3.cloned.1.call-start = ((), (), s32[]{:S(2)}) async-start(), calls=%async_computation.2 | async-start | bytes 2064384 | tf_op jit(solution)/shard_map/all_gather | solution.py:34
Sparse Core Ops, SparseCore 0:
  107.5 26.8 reduce-scatter.1
  136.1 26.9 all-gather.2
